TPU v7x, 512 devices: a whole 4x4x16 slice. The times are simulated.
512 devices in a mesh: mem: 128 (over x, y, z_lo), slab: 4 (over z_hi, core).
Axes of the slice: x: 4, y: 4, z: 16 (z_hi: 2, z_lo: 8; z = z_hi * 8 + z_lo), core: 2. Of those that a mesh axis runs over, the one named last changes fastest.
Arguments:
- prior_sample_stack: float32 [128, 3, 256, 512], P('mem', None, None, 'slab'), may hold values from -4 to 4
- obs_cell: int32 [128, 512], P('mem', 'slab'), may hold values from 0 to 255
- obs_value: float32 [128, 512], P('mem', 'slab'), may hold values from -4 to 4
- obs_bin: int32 [128, 512], P('mem', 'slab'), may hold values from 0 to 3
Outputs:
- analysis: float32 [128, 3, 256, 512], P('mem', None, None, 'slab')
Inputs may be any that keep to these rules, and one draw needn't show every extreme that they name: obs_cell is local row times 128 plus local column within the observation's region rows and its index of slab's columns.
All inputs are finite; a program needn't handle non-finite values.
Results may differ from a plain program's by a relative error of at most 0.0003.
Values sent between devices are 32-bit elements; how exact they have to be, the bound alone decides.
A program may use at most 64 MiB of HBM per device.

v0:
```python
import math

import jax
import jax.numpy as jnp
from jax import lax
from jax.sharding import PartitionSpec as P

STEPS = 12
SWEEPS = 8


time_step = 0.25
gravity = 1.0
mean_depth = 1.0
coriolis = 0.2
viscosity = 0.4
inflation = 1.1
highest = lax.Precision.HIGHEST


def padded_2(cells, sides, width):
    for axis, dim in sides:
        count = lax.axis_size(axis)
        head = lax.slice_in_dim(cells, 0, width, axis=dim)
        tail = lax.slice_in_dim(cells, cells.shape[dim] - width, cells.shape[dim], axis=dim)
        cells = jnp.concatenate(
            [
                lax.ppermute(tail, axis, [(i, (i + 1) % count) for i in range(count)]),
                cells,
                lax.ppermute(head, axis, [((i + 1) % count, i) for i in range(count)]),
            ],
            axis=dim,
        )
    return cells


def passed_along(value, axis, steps):
    count = lax.axis_size(axis)
    pairs = [(source, (source + steps) % count) for source in range(count)]
    return lax.ppermute(value, axis, pairs)


def sent_to_all(value, axis):
    size = lax.axis_size(axis)
    return lax.all_to_all(
        jnp.broadcast_to(value[None], (size, *value.shape)), axis, 0, 0, tiled=True
    )


def over_copies(value, axis):
    return sent_to_all(value, axis).sum(axis=0)


def together(arrays, axis):
    ends = [0]
    for a in arrays:
        ends.append(ends[-1] + a.size)
    running = over_copies(jnp.concatenate([a.ravel() for a in arrays]), axis)
    return tuple((running[b:e].reshape(a.shape) for a, b, e in zip(arrays, ends, ends[1:])))


def centre(values):
    return values[:, 1:-1]


def east_of(values):
    return jnp.roll(values[:, 1:-1], -1, 0)


def west_of(values):
    return jnp.roll(values[:, 1:-1], 1, 0)


def north_of(values):
    return values[:, 2:]


def south_of(values):
    return values[:, :-2]


def spread(values):
    return (
        east_of(values)
        + west_of(values)
        + north_of(values)
        + south_of(values)
        - 4.0 * centre(values)
    )


def slope_x(values):
    return 0.5 * (east_of(values) - west_of(values))


def slope_y(values):
    return 0.5 * (north_of(values) - south_of(values))


def advance(padded):
    elevation_anomaly = padded[0]
    east_wind = padded[1]
    north_wind = padded[2]
    flux_x = (mean_depth + elevation_anomaly) * east_wind
    flux_y = (mean_depth + elevation_anomaly) * north_wind
    east_mid = centre(east_wind)
    north_mid = centre(north_wind)
    new_height = centre(elevation_anomaly) + time_step * (
        viscosity * spread(elevation_anomaly) - slope_x(flux_x) - slope_y(flux_y)
    )
    new_east = east_mid + time_step * (
        viscosity * spread(east_wind)
        - east_mid * slope_x(east_wind)
        - north_mid * slope_y(east_wind)
        - gravity * slope_x(elevation_anomaly)
        + coriolis * north_mid
    )
    new_north = north_mid + time_step * (
        viscosity * spread(north_wind)
        - east_mid * slope_x(north_wind)
        - north_mid * slope_y(north_wind)
        - gravity * slope_y(elevation_anomaly)
        - coriolis * east_mid
    )
    return jnp.stack([new_height, new_east, new_north])


def partial_sums(anomaly, distance, obs_weight, innovation, band_rows):
    target = jnp.arange(band_rows).astype(jnp.float32)
    scaled_dist = (distance[None, :] - target[:, None]) / float(band_rows)
    weight = obs_weight[None, :] * jnp.exp(-0.5 * scaled_dist * scaled_dist)
    scaled = anomaly[None, :, :] * weight[:, None, :]
    gram_matrix = jnp.einsum("tmj,kj->tmk", scaled, anomaly, precision=highest)
    pull_vector = jnp.einsum("tmj,j->tm", scaled, innovation, precision=highest)
    return (gram_matrix, pull_vector)


def batch_product(left, right):
    return jnp.einsum("tij,tjk->tik", left, right, precision=highest)


def weights_from(gram_matrix, pull_vector, members):
    identity = jnp.eye(members, dtype=jnp.float32)
    gram_matrix = gram_matrix + (members - 1) / inflation * identity[None]
    traces = jnp.trace(gram_matrix, axis1=1, axis2=2)
    iterate = gram_matrix / traces[:, None, None]
    inverse = jnp.broadcast_to(identity, gram_matrix.shape)
    for iteration in range(SWEEPS):
        correction = 1.5 * identity[None] - 0.5 * batch_product(inverse, iterate)
        iterate, inverse = (batch_product(iterate, correction), batch_product(correction, inverse))
    inv_root = inverse / jnp.sqrt(traces)[:, None, None]
    inner = jnp.einsum("tij,tj->ti", inv_root, pull_vector, precision=highest)
    mean_weights = jnp.einsum("tij,tj->ti", inv_root, inner, precision=highest)
    return math.sqrt(members - 1) * inv_root + mean_weights[:, :, None]


def apply_weights(zone_portion, mixing):
    mean_state = jnp.mean(zone_portion, axis=0)
    spread_state = zone_portion - mean_state[None]
    return mean_state[None] + jnp.einsum("mftc,tmk->kftc", spread_state, mixing, precision=highest)


def local(prior_sample_stack, obs_cell, obs_value, obs_bin):
    current_condition = prior_sample_stack[0]

    def four_steps(counter, values):
        padded = padded_2(values, (("slab", 2),), 4)
        for substep in range(4):
            padded = advance(padded)
        return padded

    current_condition = lax.fori_loop(0, STEPS // 4, four_steps, current_condition)
    predicted_grid = current_condition[None]
    zone_collection = lax.all_to_all(predicted_grid, "mem", split_axis=2, concat_axis=0, tiled=True)
    heights = zone_collection[:, 0]
    members = heights.shape[0]
    band_rows = heights.shape[1]
    columns = heights.shape[2]
    observed = jnp.take(heights.reshape(members, band_rows * columns), obs_cell[0], axis=1)
    obs_mean = jnp.mean(observed, axis=0)
    anomaly = observed - obs_mean[None]
    extras = jnp.stack(
        [
            obs_value[0] - obs_mean,
            10.0 / (1.0 + obs_bin[0].astype(jnp.float32)),
            (obs_cell[0] // columns).astype(jnp.float32),
        ]
    )
    package = (anomaly, extras)
    collected = [(0, package)]
    for stride in (1, -1, 2, -2):
        collected.append((-stride, passed_along((package[0], package[1]), "mem", stride)))
    all_anomaly = jnp.concatenate([entry[1][0] for entry in collected], axis=1)
    distance = jnp.concatenate(
        [entry[1][1][2] + float(entry[0] * band_rows) for entry in collected]
    )
    obs_weight = jnp.concatenate([entry[1][1][1] for entry in collected])
    innovation = jnp.concatenate([entry[1][1][0] for entry in collected])
    gram_matrix, pull_vector = partial_sums(
        all_anomaly, distance, obs_weight, innovation, band_rows
    )
    gram_matrix, pull_vector = together((gram_matrix, pull_vector), "slab")
    mixing = weights_from(gram_matrix, pull_vector, members)
    return lax.all_to_all(
        apply_weights(zone_collection, mixing), "mem", split_axis=0, concat_axis=2, tiled=True
    )


def solution(mesh):
    placed = (P("mem", None, None, "slab"), P("mem", "slab"), P("mem", "slab"), P("mem", "slab"))
    return jax.shard_map(
        local, mesh=mesh, in_specs=placed, out_specs=P("mem", None, None, "slab"), check_vma=False
    )
```

profile of v0, /device:TPU:1, one launch (start us, length us, event | category | flops | bytes accessed | tf_op | source)
XLA Modules:
  0.0 343.0 jit_solution(7744454603862353869)
XLA Ops:
  1.0 111.7 %while.10 = (s32[]{:T(128)}, f32[3,256,128]{2,1,0:T(8,128)S(1)}, s32[]{:T(128)}) while((s32[]{:T(128)}, f32[3,256,128]{2,1,0:T(8,128)S(1)}, s32[]{:T(128)}) %tuple.159), condition=%wide.region_1.2_spmd, body=%wide.region_0.1_spmd.sunk | while | flops 9566210 | bytes 27316348 | solution.py:172
  1.2 8.7 %collective-permute-start = (f32[3,256,4]{2,1,0:T(8,128)S(1)}, f32[3,256,4]{2,1,0:T(8,128)S(1)}, u32[]{:S(2)}, u32[]{:S(2)}) collective-permute-start(f32[3,256,4]{2,1,0:T(8,128)S(1)} %get-tuple-element.233), channel_id=1, source_target_pairs={{1,0},{2,1},{3,2},{0,3},{5,4},{6,5},{7,6},{4,7},{9,8},{10,9},{11,1... | collective-permute-start | bytes 36872 | tf_op jit(solution)/shard_map/while/body/eval_jaxpr/ppermute | solution.py:30
  9.9 10.0 %collective-permute-start.1 = (f32[3,256,4]{2,1,0:T(8,128)S(1)}, f32[3,256,4]{2,1,0:T(8,128)S(1)}, u32[]{:S(2)}, u32[]{:S(2)}) collective-permute-start(f32[3,256,4]{2,1,0:T(8,128)S(1)} %get-tuple-element.234), channel_id=1, source_target_pairs={{0,1},{1,2},{2,3},{3,0},{4,5},{5,6},{6,7},{7,4},{8,9},{9,10},{10,1... | collective-permute-start | bytes 36872 | tf_op jit(solution)/shard_map/while/body/eval_jaxpr/ppermute | solution.py:28
  19.9 3.8 %collective-permute-done = f32[3,256,4]{2,1,0:T(8,128)S(1)} collective-permute-done((f32[3,256,4]{2,1,0:T(8,128)S(1)}, f32[3,256,4]{2,1,0:T(8,128)S(1)}, u32[]{:S(2)}, u32[]{:S(2)}) %collective-permute-start) | collective-permute-done | bytes 12320 | tf_op jit(solution)/shard_map/while/body/eval_jaxpr/ppermute | solution.py:30
  23.7 18.3 %collective-permute-done.1 = f32[3,256,4]{2,1,0:T(8,128)S(1)} collective-permute-done((f32[3,256,4]{2,1,0:T(8,128)S(1)}, f32[3,256,4]{2,1,0:T(8,128)S(1)}, u32[]{:S(2)}, u32[]{:S(2)}) %collective-permute-start.1) | collective-permute-done | bytes 12320 | tf_op jit(solution)/shard_map/while/body/eval_jaxpr/ppermute | solution.py:28
  50.1 3.3 collective-permute-start
  53.4 11.9 %collective-permute-start.1 = (f32[3,256,4]{2,1,0:T(8,128)S(1)}, f32[3,256,4]{2,1,0:T(8,128)S(1)}, u32[]{:S(2)}, u32[]{:S(2)}) collective-permute-start(f32[3,256,4]{2,1,0:T(8,128)S(1)} %get-tuple-element.234), channel_id=1, source_target_pairs={{0,1},{1,2},{2,3},{3,0},{4,5},{5,6},{6,7},{7,4},{8,9},{9,10},{10,1... | collective-permute-start | bytes 36872 | tf_op jit(solution)/shard_map/while/body/eval_jaxpr/ppermute | solution.py:28
  65.4 11.8 %collective-permute-done = f32[3,256,4]{2,1,0:T(8,128)S(1)} collective-permute-done((f32[3,256,4]{2,1,0:T(8,128)S(1)}, f32[3,256,4]{2,1,0:T(8,128)S(1)}, u32[]{:S(2)}, u32[]{:S(2)}) %collective-permute-start) | collective-permute-done | bytes 12320 | tf_op jit(solution)/shard_map/while/body/eval_jaxpr/ppermute | solution.py:30
  85.2 5.1 %collective-permute-start = (f32[3,256,4]{2,1,0:T(8,128)S(1)}, f32[3,256,4]{2,1,0:T(8,128)S(1)}, u32[]{:S(2)}, u32[]{:S(2)}) collective-permute-start(f32[3,256,4]{2,1,0:T(8,128)S(1)} %get-tuple-element.233), channel_id=1, source_target_pairs={{1,0},{2,1},{3,2},{0,3},{5,4},{6,5},{7,6},{4,7},{9,8},{10,9},{11,1... | collective-permute-start | bytes 36872 | tf_op jit(solution)/shard_map/while/body/eval_jaxpr/ppermute | solution.py:30
  90.3 9.4 %collective-permute-start.1 = (f32[3,256,4]{2,1,0:T(8,128)S(1)}, f32[3,256,4]{2,1,0:T(8,128)S(1)}, u32[]{:S(2)}, u32[]{:S(2)}) collective-permute-start(f32[3,256,4]{2,1,0:T(8,128)S(1)} %get-tuple-element.234), channel_id=1, source_target_pairs={{0,1},{1,2},{2,3},{3,0},{4,5},{5,6},{6,7},{7,4},{8,9},{9,10},{10,1... | collective-permute-start | bytes 36872 | tf_op jit(solution)/shard_map/while/body/eval_jaxpr/ppermute | solution.py:28
  99.7 5.1 %collective-permute-done = f32[3,256,4]{2,1,0:T(8,128)S(1)} collective-permute-done((f32[3,256,4]{2,1,0:T(8,128)S(1)}, f32[3,256,4]{2,1,0:T(8,128)S(1)}, u32[]{:S(2)}, u32[]{:S(2)}) %collective-permute-start) | collective-permute-done | bytes 12320 | tf_op jit(solution)/shard_map/while/body/eval_jaxpr/ppermute | solution.py:30
  113.9 47.4 %all-to-all-start = ((f32[1,3,256,128]{3,0,1,2:T(1,128)}), f32[1,3,256,128]{3,0,1,2:T(1,128)S(1)}, u32[]{:S(2)}, u32[]{:S(2)}) async-start(f32[1,3,256,128]{3,0,1,2:T(1,128)} %copy.44), calls=%async_computation | async-start | bytes 786432 | tf_op jit(solution)/shard_map/all_to_all | solution.py:174
  162.6 23.9 %all-to-all-done = f32[1,3,256,128]{3,0,1,2:T(1,128)S(1)} async-done(((f32[1,3,256,128]{3,0,1,2:T(1,128)}), f32[1,3,256,128]{3,0,1,2:T(1,128)S(1)}, u32[]{:S(2)}, u32[]{:S(2)}) %all-to-all-start) | async-done | bytes 393248 | tf_op jit(solution)/shard_map/all_to_all | solution.py:174
  188.2 2.6 collective-permute-start.6
  190.8 13.5 %collective-permute-start.7 = (f32[3,128]{1,0:T(4,128)S(1)}, f32[3,128]{1,0:T(4,128)S(1)}, u32[]{:S(2)}, u32[]{:S(2)}) collective-permute-start(f32[3,128]{1,0:T(4,128)S(1)} %pad_maximum_fusion.27), channel_id=1, source_target_pairs={{0,508},{4,0},{8,4},{12,8},{16,12},{20,16},{24,20},{28,24},{32,28}... | collective-permute-start | bytes 4616 | tf_op jit(solution)/shard_map/ppermute | solution.py:40
  204.3 1.9 collective-permute-start.8
  206.2 13.3 %collective-permute-start.9 = (f32[3,128]{1,0:T(4,128)S(1)}, f32[3,128]{1,0:T(4,128)S(1)}, u32[]{:S(2)}, u32[]{:S(2)}) collective-permute-start(f32[3,128]{1,0:T(4,128)S(1)} %pad_maximum_fusion.27), channel_id=1, source_target_pairs={{0,504},{4,508},{8,0},{12,4},{16,8},{20,12},{24,16},{28,20},{32,24... | collective-permute-start | bytes 4616 | tf_op jit(solution)/shard_map/ppermute | solution.py:40
  219.5 1.9 collective-permute-start.2
  221.5 14.2 %collective-permute-start.3 = (f32[128,128]{1,0:T(8,128)S(1)}, f32[128,128]{1,0:T(8,128)S(1)}, u32[]{:S(2)}, u32[]{:S(2)}) collective-permute-start(f32[128,128]{1,0:T(8,128)S(1)} %get-tuple-element.38), channel_id=1, source_target_pairs={{0,508},{4,0},{8,4},{12,8},{16,12},{20,16},{24,20},{28,24},{32,28}... | collective-permute-start | bytes 196616 | tf_op jit(solution)/shard_map/ppermute | solution.py:40
  235.7 1.9 collective-permute-start.4
  237.7 13.3 %collective-permute-start.5 = (f32[128,128]{1,0:T(8,128)S(1)}, f32[128,128]{1,0:T(8,128)S(1)}, u32[]{:S(2)}, u32[]{:S(2)}) collective-permute-start(f32[128,128]{1,0:T(8,128)S(1)} %get-tuple-element.38), channel_id=1, source_target_pairs={{0,504},{4,508},{8,0},{12,4},{16,8},{20,12},{24,16},{28,20},{32,24... | collective-permute-start | bytes 196616 | tf_op jit(solution)/shard_map/ppermute | solution.py:40
  254.8 20.6 %all-to-all-start.1 = ((f32[4,1,33024]{2,1,0:T(1,128)}), f32[4,1,33024]{2,1,0:T(1,128)S(1)}, u32[]{:S(2)}, u32[]{:S(2)}) async-start(f32[4,1,33024]{2,1,0:T(1,128)} %broadcast_in_dim.31), calls=%async_computation.1 | async-start | bytes 1056768 | tf_op jit(solution)/shard_map/all_to_all | solution.py:45
  275.4 16.5 %all-to-all-done.1 = f32[4,1,33024]{2,1,0:T(1,128)S(1)} async-done(((f32[4,1,33024]{2,1,0:T(1,128)}), f32[4,1,33024]{2,1,0:T(1,128)S(1)}, u32[]{:S(2)}, u32[]{:S(2)}) %all-to-all-start.1) | async-done | bytes 528416 | tf_op jit(solution)/shard_map/all_to_all | solution.py:45
  301.3 40.8 %all_to_all.42 = f32[128,3,2,128]{3,2,1,0:T(2,128)S(1)} all-to-all(f32[128,3,2,128]{3,2,1,0:T(2,128)S(1)} %copy.51), channel_id=1, replica_groups=mesh['mem'=128,'slab'=4] {'mem'}, dimensions={0} | all-to-all | bytes 786432 | tf_op jit(solution)/shard_map/all_to_all | solution.py:204
  (222 shorter events, 42.6 us)
Async XLA Ops:
  0.0 1.0 copy-start
  1.2 22.6 %collective-permute-start = (f32[3,256,4]{2,1,0:T(8,128)S(1)}, f32[3,256,4]{2,1,0:T(8,128)S(1)}, u32[]{:S(2)}, u32[]{:S(2)}) collective-permute-start(f32[3,256,4]{2,1,0:T(8,128)S(1)} %get-tuple-element.233), channel_id=1, source_target_pairs={{1,0},{2,1},{3,2},{0,3},{5,4},{6,5},{7,6},{4,7},{9,8},{10,9},{11,1... | collective-permute-start | bytes 36872 | tf_op jit(solution)/shard_map/while/body/eval_jaxpr/ppermute | solution.py:30
  9.9 32.1 %collective-permute-start.1 = (f32[3,256,4]{2,1,0:T(8,128)S(1)}, f32[3,256,4]{2,1,0:T(8,128)S(1)}, u32[]{:S(2)}, u32[]{:S(2)}) collective-permute-start(f32[3,256,4]{2,1,0:T(8,128)S(1)} %get-tuple-element.234), channel_id=1, source_target_pairs={{0,1},{1,2},{2,3},{3,0},{4,5},{5,6},{6,7},{7,4},{8,9},{9,10},{10,1... | collective-permute-start | bytes 36872 | tf_op jit(solution)/shard_map/while/body/eval_jaxpr/ppermute | solution.py:28
  50.1 27.0 %collective-permute-start = (f32[3,256,4]{2,1,0:T(8,128)S(1)}, f32[3,256,4]{2,1,0:T(8,128)S(1)}, u32[]{:S(2)}, u32[]{:S(2)}) collective-permute-start(f32[3,256,4]{2,1,0:T(8,128)S(1)} %get-tuple-element.233), channel_id=1, source_target_pairs={{1,0},{2,1},{3,2},{0,3},{5,4},{6,5},{7,6},{4,7},{9,8},{10,9},{11,1... | collective-permute-start | bytes 36872 | tf_op jit(solution)/shard_map/while/body/eval_jaxpr/ppermute | solution.py:30
  53.4 23.7 %collective-permute-start.1 = (f32[3,256,4]{2,1,0:T(8,128)S(1)}, f32[3,256,4]{2,1,0:T(8,128)S(1)}, u32[]{:S(2)}, u32[]{:S(2)}) collective-permute-start(f32[3,256,4]{2,1,0:T(8,128)S(1)} %get-tuple-element.234), channel_id=1, source_target_pairs={{0,1},{1,2},{2,3},{3,0},{4,5},{5,6},{6,7},{7,4},{8,9},{9,10},{10,1... | collective-permute-start | bytes 36872 | tf_op jit(solution)/shard_map/while/body/eval_jaxpr/ppermute | solution.py:28
  85.2 19.6 %collective-permute-start = (f32[3,256,4]{2,1,0:T(8,128)S(1)}, f32[3,256,4]{2,1,0:T(8,128)S(1)}, u32[]{:S(2)}, u32[]{:S(2)}) collective-permute-start(f32[3,256,4]{2,1,0:T(8,128)S(1)} %get-tuple-element.233), channel_id=1, source_target_pairs={{1,0},{2,1},{3,2},{0,3},{5,4},{6,5},{7,6},{4,7},{9,8},{10,9},{11,1... | collective-permute-start | bytes 36872 | tf_op jit(solution)/shard_map/while/body/eval_jaxpr/ppermute | solution.py:30
  90.3 14.5 %collective-permute-start.1 = (f32[3,256,4]{2,1,0:T(8,128)S(1)}, f32[3,256,4]{2,1,0:T(8,128)S(1)}, u32[]{:S(2)}, u32[]{:S(2)}) collective-permute-start(f32[3,256,4]{2,1,0:T(8,128)S(1)} %get-tuple-element.234), channel_id=1, source_target_pairs={{0,1},{1,2},{2,3},{3,0},{4,5},{5,6},{6,7},{7,4},{8,9},{9,10},{10,1... | collective-permute-start | bytes 36872 | tf_op jit(solution)/shard_map/while/body/eval_jaxpr/ppermute | solution.py:28
  113.9 72.7 %all-to-all-start = ((f32[1,3,256,128]{3,0,1,2:T(1,128)}), f32[1,3,256,128]{3,0,1,2:T(1,128)S(1)}, u32[]{:S(2)}, u32[]{:S(2)}) async-start(f32[1,3,256,128]{3,0,1,2:T(1,128)} %copy.44), calls=%async_computation | async-start | bytes 786432 | tf_op jit(solution)/shard_map/all_to_all | solution.py:174
  161.3 0.7 copy-start.3
  162.0 0.7 copy-start.4
  187.5 0.7 copy-start.2
  188.2 33.3 %collective-permute-start.6 = (f32[3,128]{1,0:T(4,128)S(1)}, f32[3,128]{1,0:T(4,128)S(1)}, u32[]{:S(2)}, u32[]{:S(2)}) collective-permute-start(f32[3,128]{1,0:T(4,128)S(1)} %pad_maximum_fusion.27), channel_id=1, source_target_pairs={{0,4},{4,8},{8,12},{12,16},{16,20},{20,24},{24,28},{28,32},{32,36}... | collective-permute-start | bytes 4616 | tf_op jit(solution)/shard_map/ppermute | solution.py:40
  190.8 44.9 %collective-permute-start.7 = (f32[3,128]{1,0:T(4,128)S(1)}, f32[3,128]{1,0:T(4,128)S(1)}, u32[]{:S(2)}, u32[]{:S(2)}) collective-permute-start(f32[3,128]{1,0:T(4,128)S(1)} %pad_maximum_fusion.27), channel_id=1, source_target_pairs={{0,508},{4,0},{8,4},{12,8},{16,12},{20,16},{24,20},{28,24},{32,28}... | collective-permute-start | bytes 4616 | tf_op jit(solution)/shard_map/ppermute | solution.py:40
  204.3 33.4 %collective-permute-start.8 = (f32[3,128]{1,0:T(4,128)S(1)}, f32[3,128]{1,0:T(4,128)S(1)}, u32[]{:S(2)}, u32[]{:S(2)}) collective-permute-start(f32[3,128]{1,0:T(4,128)S(1)} %pad_maximum_fusion.27), channel_id=1, source_target_pairs={{0,8},{4,12},{8,16},{12,20},{16,24},{20,28},{24,32},{28,36},{32,40... | collective-permute-start | bytes 4616 | tf_op jit(solution)/shard_map/ppermute | solution.py:40
  206.2 44.8 %collective-permute-start.9 = (f32[3,128]{1,0:T(4,128)S(1)}, f32[3,128]{1,0:T(4,128)S(1)}, u32[]{:S(2)}, u32[]{:S(2)}) collective-permute-start(f32[3,128]{1,0:T(4,128)S(1)} %pad_maximum_fusion.27), channel_id=1, source_target_pairs={{0,504},{4,508},{8,0},{12,4},{16,8},{20,12},{24,16},{28,20},{32,24... | collective-permute-start | bytes 4616 | tf_op jit(solution)/shard_map/ppermute | solution.py:40
  219.5 31.6 %collective-permute-start.2 = (f32[128,128]{1,0:T(8,128)S(1)}, f32[128,128]{1,0:T(8,128)S(1)}, u32[]{:S(2)}, u32[]{:S(2)}) collective-permute-start(f32[128,128]{1,0:T(8,128)S(1)} %get-tuple-element.38), channel_id=1, source_target_pairs={{0,4},{4,8},{8,12},{12,16},{16,20},{20,24},{24,28},{28,32},{32,36}... | collective-permute-start | bytes 196616 | tf_op jit(solution)/shard_map/ppermute | solution.py:40
  221.5 29.6 %collective-permute-start.3 = (f32[128,128]{1,0:T(8,128)S(1)}, f32[128,128]{1,0:T(8,128)S(1)}, u32[]{:S(2)}, u32[]{:S(2)}) collective-permute-start(f32[128,128]{1,0:T(8,128)S(1)} %get-tuple-element.38), channel_id=1, source_target_pairs={{0,508},{4,0},{8,4},{12,8},{16,12},{20,16},{24,20},{28,24},{32,28}... | collective-permute-start | bytes 196616 | tf_op jit(solution)/shard_map/ppermute | solution.py:40
  235.7 15.5 %collective-permute-start.4 = (f32[128,128]{1,0:T(8,128)S(1)}, f32[128,128]{1,0:T(8,128)S(1)}, u32[]{:S(2)}, u32[]{:S(2)}) collective-permute-start(f32[128,128]{1,0:T(8,128)S(1)} %get-tuple-element.38), channel_id=1, source_target_pairs={{0,8},{4,12},{8,16},{12,20},{16,24},{20,28},{24,32},{28,36},{32,40... | collective-permute-start | bytes 196616 | tf_op jit(solution)/shard_map/ppermute | solution.py:40
  237.7 14.6 %collective-permute-start.5 = (f32[128,128]{1,0:T(8,128)S(1)}, f32[128,128]{1,0:T(8,128)S(1)}, u32[]{:S(2)}, u32[]{:S(2)}) collective-permute-start(f32[128,128]{1,0:T(8,128)S(1)} %get-tuple-element.38), channel_id=1, source_target_pairs={{0,504},{4,508},{8,0},{12,4},{16,8},{20,12},{24,16},{28,20},{32,24... | collective-permute-start | bytes 196616 | tf_op jit(solution)/shard_map/ppermute | solution.py:40
  254.8 37.2 %all-to-all-start.1 = ((f32[4,1,33024]{2,1,0:T(1,128)}), f32[4,1,33024]{2,1,0:T(1,128)S(1)}, u32[]{:S(2)}, u32[]{:S(2)}) async-start(f32[4,1,33024]{2,1,0:T(1,128)} %broadcast_in_dim.31), calls=%async_computation.1 | async-start | bytes 1056768 | tf_op jit(solution)/shard_map/all_to_all | solution.py:45
  292.4 6.1 %copy-start.1 = (f32[33024]{0:T(1024)}, f32[33024]{0:T(1024)S(1)}, u32[]{:S(2)}) copy-start(f32[33024]{0:T(1024)S(1)} %reduce_sum.39) | copy-start | bytes 396292
  299.1 0.7 slice-start
where the time goes:
time: 344 us; the launch traced here: 343 us
  starting transfers between devices  179 us (52%)
  waiting for transfers between devices  80.5 us (23%)
  blocking collectives  40.8 us (12%)
  local copies, waits for them, and re-layouts  20.2 us (6%)
  other arithmetic  12.4 us (4%)
  matrix products  8.88 us (3%)
    ppermute x8, starting transfers between devices, passed_along(): return lax.ppermute(value, axis, pairs)  62.6 us
    all_to_all x1, starting transfers between devices, local(): lax.all_to_all(predicted_grid, 'mem', split_axis=2, concat_axis=0, tiled=...  47.4 us
    all_to_all x1, blocking collectives, local(): lax.all_to_all(apply_weights(zone_collection, mixing), 'mem', split_axis=...  40.8 us
    ppermute x3, starting transfers between devices, padded_2(): lax.ppermute(tail, axis, [(i, (i + 1) % count) for i in range(count)])  31.3 us
    all_to_all x1, waiting for transfers between devices, local(): lax.all_to_all(predicted_grid, 'mem', split_axis=2, concat_axis=0, tiled=...  23.9 us
    ppermute x3, waiting for transfers between devices, padded_2(): lax.ppermute(head, axis, [((i + 1) % count, i) for i in range(count)])  20.7 us
    all_to_all x1, starting transfers between devices, sent_to_all(): lax.all_to_all(jnp.broadcast_to(value[None], (size, *value.shape)), axis,...  20.6 us
    ppermute x3, waiting for transfers between devices, padded_2(): lax.ppermute(tail, axis, [(i, (i + 1) % count) for i in range(count)])  18.3 us
  transfers between devices with their start and end apart: 16, of which 7 were waited for; matrix products, arithmetic and copies ran while one was open for 0% of the time, Pallas kernels for 0%

commit v1 on v0

v1 whole, which is shorter than its diff:
```python
import math

import jax
import jax.numpy as jnp
from jax import lax
from jax.experimental import pallas as pl
from jax.experimental.pallas import tpu as pltpu
from jax.sharding import PartitionSpec as P

STEPS = 12
SWEEPS = 8
SIZE = 32
BATCH = (16, 16, 16)
MESH = pl.DeviceIdType.MESH
F32 = jnp.float32
BF16 = jnp.bfloat16

BASE = 24
ROWS = BASE + 128 + BASE
OFFSETS = (1, -1, 2, -2)
ORDER = (0, 7, 1, 6, 2, 5, 3, 4)


def device_of(x, y, z, core):
    return ((x * 4 + y) * 8 + z % 8, (z // 8) * 2 + core)


def region_at(x, y, k):
    pos = y * 4 + x + (y % 2) * (3 - 2 * x)
    pos = pos + (k % 2) * (15 - 2 * pos)
    return k * 16 + pos


def place_of(region):
    k, pos = region // 16, region % 16
    pos = pos + (k % 2) * (15 - 2 * pos)
    y, x = pos // 4, pos % 4
    return x + (y % 2) * (3 - 2 * x), y, k


def halves(a):
    hi = a.astype(BF16)
    return hi, (a - hi.astype(F32)).astype(BF16)


def as_lhs(a):
    return jnp.concatenate(halves(a), axis=1)


def as_rhs(b):
    row = jnp.concatenate(halves(b), axis=1)
    return jnp.concatenate([row, row], axis=0)


def product(lhs, rhs):
    r = jnp.dot(lhs, rhs, preferred_element_type=F32)
    return r[:, :128] + r[:, 128:]


def forecast_block(src, dst, row, size):
    c, n, s = {}, {}, {}
    for f in range(3):
        for t in range(2):
            c[f, t] = src[f, t, row : row + size]
            n[f, t] = src[f, t, row + 1 : row + 1 + size]
            s[f, t] = src[f, t, row - 1 : row - 1 + size]
    for t in range(2):
        if t == 0:
            e = [c[f, 1] for f in range(3)]
            w = [pltpu.roll(c[f, 1], 1, 1) for f in range(3)]
        else:
            e = [pltpu.roll(c[f, 0], 127, 1) for f in range(3)]
            w = [c[f, 0] for f in range(3)]
        h, u, v = (c[f, t] for f in range(3))
        hn, un, vn = (n[f, t] for f in range(3))
        hs, us, vs = (s[f, t] for f in range(3))
        he, ue, ve = e
        hw, uw, vw = w
        flux = (1.0 + he) * ue - (1.0 + hw) * uw + (1.0 + hn) * vn - (1.0 + hs) * vs
        a, b = 0.125 * u, 0.125 * v
        dst[0, t, row : row + size] = 0.6 * h + 0.1 * (he + hw + hn + hs) - 0.125 * flux
        dst[1, t, row : row + size] = (
            0.6 * u + 0.1 * (ue + uw + un + us) - (a * (ue - uw) + b * (un - us)) - 0.125 * (he - hw) + 0.05 * v
        )
        dst[2, t, row : row + size] = (
            0.6 * v + 0.1 * (ve + vw + vn + vs) - (a * (ve - vw) + b * (vn - vs)) - 0.125 * (hn - hs) - 0.05 * u
        )


def kernel(
    prior, cell, value, bins, out,
    nat, state, halo_out, halo_in, obs_out, obs_in, heights_out, winds_out, heights, winds,
    parts, parts_in, chunk, chunk_in, grams, back_out, back,
    load_sem, halo_send, halo_recv, obs_send, obs_recv, a2a_send, a2a_recv,
    part_send, part_recv, chunk_send, chunk_recv, gram_send, gram_recv, lines,
):
    m, slab = lax.axis_index("mem"), lax.axis_index("slab")
    x, y, zl = m // 32, (m // 8) % 4, m % 8
    z_hi, core = slab // 2, slab % 2
    z = z_hi * 8 + zl
    k, par = z // 2, z % 2
    region = region_at(x, y, k)
    ident = par * 2 + core
    away = (z_hi + par) % 2

    def remote(src, dst, send, recv, where):
        return pltpu.make_async_remote_copy(
            src_ref=src, dst_ref=dst, send_sem=send, recv_sem=recv, device_id=where, device_id_type=MESH
        )

    def group(i):
        return device_of(x, y, 2 * k + i // 2, i % 2)

    def neighbour(o):
        nx, ny, nk = place_of((region + o + 128) % 128)
        return device_of(nx, ny, 2 * nk + par, core)

    load = pltpu.make_async_copy(prior, nat, load_sem)
    load.start()

    barrier = pltpu.get_barrier_semaphore()

    def greet(where):
        pl.semaphore_signal(barrier, inc=1, device_id=where, device_id_type=MESH)

    for side in (1, 3):
        greet((m, (slab + side) % 4))
    for j in range(1, 4):
        greet(group((ident + j) % 4))
    for o in OFFSETS:
        greet(neighbour(o))

    def in_plane(j):
        return ((x + j % 4) % 4 * 4 + (y + j // 4) % 4) * 8 + zl, slab

    def greet_line_and_plane(j, carry):
        pz = (z + j) % 16
        greet((m - zl + pz % 8, (pz // 8) * 2 + core))
        greet(in_plane(j))
        return carry

    def tell_plane(j, carry):
        pl.semaphore_signal(lines, inc=1, device_id=in_plane(j), device_id_type=MESH)
        return carry

    lax.fori_loop(1, 16, greet_line_and_plane, 0)
    load.wait()
    for f in range(3):
        for t in range(2):
            state[0, f, t, BASE : BASE + 128] = nat[f, pl.ds(t, 128, stride=2), :].T
            i = (f * 2 + t) * 12
            halo_out[0, i : i + 12] = state[0, f, t, BASE : BASE + 12]
            halo_out[1, i : i + 12] = state[0, f, t, BASE + 116 : BASE + 128]
    halo = [
        remote(halo_out.at[0], halo_in.at[0], halo_send.at[0], halo_recv.at[0], (m, (slab + 3) % 4)),
        remote(halo_out.at[1], halo_in.at[1], halo_send.at[1], halo_recv.at[1], (m, (slab + 1) % 4)),
    ]

    pl.semaphore_wait(barrier, 39)
    for copy in halo:
        copy.start()
    lax.fori_loop(1, 16, tell_plane, 0)

    for copy in halo:
        copy.wait()
    for f in range(3):
        for t in range(2):
            i = (f * 2 + t) * 12
            state[0, f, t, BASE + 128 : BASE + 140] = halo_in[0, i : i + 12]
            state[0, f, t, BASE - 12 : BASE] = halo_in[1, i : i + 12]

    def two_steps(counter, carry):
        for now in range(2):
            for block in range(160 // SIZE):
                forecast_block(state.at[now], state.at[1 - now], BASE - 16 + SIZE * block, SIZE)
        return carry

    lax.fori_loop(0, STEPS // 2, two_steps, 0)

    pl.semaphore_wait(lines, 15)

    ox, oy, ok = place_of(m)
    obs_out[0:1] = cell[...].astype(F32)
    obs_out[1:2] = value[...]
    obs_out[2:3] = bins[...].astype(F32)
    obs_where = device_of(ox, oy, 2 * ok + z_hi, core)
    obs_copy = remote(obs_out, obs_in, obs_send, obs_recv, obs_where)
    obs_home = jnp.logical_and(obs_where[0] == m, obs_where[1] == slab)

    @pl.when(jnp.logical_not(obs_home))
    def _():
        obs_copy.start()

    @pl.when(obs_home)
    def _():
        obs_in[...] = obs_out[...]

    for t in range(2):
        heights_out[:, t, :] = state[0, 0, t, BASE : BASE + 128].T
    for f in range(1, 3):
        for t in range(2):
            winds_out[:, 2 * f - 2 + t, :] = state[0, f, t, BASE : BASE + 128].T

    def send_regions(first, last, mine, theirs, send, recv):
        def body(xy, carry):
            px, py = (x + xy % 4) % 4, (y + xy // 4) % 4
            pos = py * 4 + px + (py % 2) * (3 - 2 * px)
            column = (px * 4 + py) * 8
            for j, d in enumerate(ORDER):
                zk = (k + away * 4 + d) % 8
                pz = 2 * zk + z_hi
                to_region = zk * 16 + pos + (zk % 2) * (15 - 2 * pos)
                where = (column + pz % 8, (pz // 8) * 2 + core)
                copy = remote(mine.at[to_region], theirs.at[m], send, recv, where)
                if j == 0:
                    pl.when(xy + away > 0)(copy.start)
                else:
                    copy.start()
            return carry

        if first < last:
            lax.fori_loop(first, last, body, 0)

    def send_winds(first, last):
        send_regions(first, last, winds_out, winds, a2a_send.at[1], a2a_recv.at[1])

    send_regions(0, 16, heights_out, heights, a2a_send.at[0], a2a_recv.at[0])
    send_winds(0, BATCH[0])

    @pl.when(away == 0)
    def _():
        heights[m] = heights_out[region]
        winds[m] = winds_out[region]

    here = (m, slab)

    def wait_all(source, target, send, recv):
        home = remote(source.at[0:127], target.at[0:127], send, recv, here)
        full = remote(source, target, send, recv, here)
        return home, full

    def wait_recv(pair):
        pl.when(away == 0)(pair[0].wait_recv)
        pl.when(away == 1)(pair[1].wait_recv)

    def wait_send(pair):
        pl.when(away == 0)(pair[0].wait_send)
        pl.when(away == 1)(pair[1].wait_send)

    height_wait = wait_all(heights_out, heights, a2a_send.at[0], a2a_recv.at[0])
    wind_wait = wait_all(winds_out, winds, a2a_send.at[1], a2a_recv.at[1])

    @pl.when(jnp.logical_not(obs_home))
    def _():
        obs_copy.wait()

    where_cell = obs_in[0:1]
    picked = lax.broadcasted_iota(jnp.int32, (256, 128), 0).astype(F32) == where_cell
    picked = picked.astype(F32).astype(BF16)
    wait_recv(height_wait)
    field = {}
    for t in range(2):
        field[0, t] = heights[:, t, :]
    flat = jnp.concatenate([field[0, 0], field[0, 1]], axis=1)
    hi = flat.astype(BF16)
    rest = flat - hi.astype(F32)
    mid = rest.astype(BF16)
    low = (rest - mid.astype(F32)).astype(BF16)
    observed = (
        jnp.dot(hi, picked, preferred_element_type=F32)
        + jnp.dot(mid, picked, preferred_element_type=F32)
        + jnp.dot(low, picked, preferred_element_type=F32)
    )
    obs_mean = jnp.mean(observed, axis=0, keepdims=True)
    anomaly = observed - obs_mean
    innovation = obs_in[1:2] - obs_mean
    weight = 10.0 / (1.0 + obs_in[2:3])
    upper = (where_cell >= 128.0).astype(F32)
    by_row = (weight * (1.0 - upper), weight * upper)
    lhs = jnp.concatenate(
        [anomaly * by_row[0], anomaly * by_row[1], jnp.broadcast_to(innovation * by_row[0], (8, 128)),
         jnp.broadcast_to(innovation * by_row[1], (8, 128))], axis=0
    )
    ah, al = halves(anomaly)
    rhs = jnp.concatenate([jnp.concatenate([ah, ah], axis=1), jnp.concatenate([al, al], axis=1)], axis=0)
    sums = lax.dot_general(as_lhs(lhs), rhs, (((1,), (1,)), ((), ())), preferred_element_type=F32)
    sums = sums[:, :128] + sums[:, 128:]
    pulls = jnp.concatenate([sums[256:260], sums[264:268]], axis=0)
    for i in range(4):
        parts[i, 0:32] = sums[32 * i : 32 * i + 32]
        parts[i, 32:64] = sums[128 + 32 * i : 160 + 32 * i]
        parts[i, 64:72] = pulls

    part_copies = []
    for j in range(1, 4):
        other = (ident + j) % 4
        part_copies.append(
            remote(parts.at[other], parts_in.at[j - 1], part_send.at[j - 1], part_recv.at[j - 1], group(other))
        )
        part_copies[-1].start()
    send_winds(BATCH[0], BATCH[1])
    for copy in part_copies:
        copy.wait()
    chunk[...] = (parts[ident] + parts_in[0]) + (parts_in[1] + parts_in[2])

    chunk_copies = []
    for j, o in enumerate(OFFSETS):
        chunk_copies.append(remote(chunk, chunk_in.at[j], chunk_send.at[j], chunk_recv.at[j], neighbour(o)))
        chunk_copies[-1].start()
    send_winds(BATCH[1], BATCH[2])
    for copy in chunk_copies:
        copy.wait()

    pull = []
    for t in range(2):
        total, row = 0.0, 0.0
        for j, o in enumerate((0,) + OFFSETS):
            source = chunk if j == 0 else chunk_in.at[j - 1]
            for q in range(2):
                scale = math.exp(-0.5 * ((-2 * o + q - t) / 2.0) ** 2)
                total = total + scale * source[32 * q : 32 * q + 32]
                row = row + scale * source[64 + 4 * q : 65 + 4 * q]
        grams[ident, 32 * t : 32 * t + 32] = total
        pull.append(row)
    gram_copies = []
    for j in range(1, 4):
        other = (ident + j) % 4
        gram_copies.append(
            remote(grams.at[ident], grams.at[ident], gram_send.at[j - 1], gram_recv.at[j - 1], group(other))
        )
        gram_copies[-1].start()
    send_winds(BATCH[2], 16)
    for copy in gram_copies:
        copy.wait()

    r_id = lax.broadcasted_iota(jnp.int32, (128, 128), 0)
    c_id = lax.broadcasted_iota(jnp.int32, (128, 128), 1)
    eye = (r_id == c_id).astype(F32)
    ys, zs, scales = [], [], []
    for t in range(2):
        g = jnp.concatenate([grams[i, 32 * t : 32 * t + 32] for i in range(4)], axis=0)
        g = g + (127.0 / 1.1) * eye
        trace = jnp.sum(jnp.sum(g * eye, axis=0, keepdims=True), axis=1, keepdims=True)
        scales.append(trace)
        ys.append(g / trace)
        zs.append(None)
    for sweep in range(SWEEPS):
        for t in range(2):
            if sweep == 0:
                correction = 1.5 * eye - 0.5 * ys[t]
                ys[t] = product(as_lhs(ys[t]), as_rhs(correction))
                zs[t] = correction
            else:
                correction = 1.5 * eye - 0.5 * product(as_lhs(zs[t]), as_rhs(ys[t]))
                if sweep < SWEEPS - 1:
                    both = product(
                        jnp.concatenate([as_lhs(ys[t]), as_lhs(zs[t])], axis=0), as_rhs(correction)
                    )
                    ys[t], zs[t] = both[:128], both[128:]
                else:
                    zs[t] = product(as_lhs(zs[t]), as_rhs(correction))

    mixers = []
    for t in range(2):
        z_rhs = as_rhs(zs[t])
        row = jnp.broadcast_to(pull[t], (8, 128))
        row = product(as_lhs(row), z_rhs)
        row = product(as_lhs(row), z_rhs)[0:1] / scales[t]
        mixers.append(as_lhs(zs[t] * (math.sqrt(127.0) * lax.rsqrt(scales[t])) + row))

    wait_recv(wind_wait)
    for f in range(1, 3):
        for t in range(2):
            field[f, t] = winds[:, 2 * f - 2 + t, :]
    for f in range(3):
        for t in range(2):
            mean = jnp.mean(field[f, t], axis=0, keepdims=True)
            back_out[:, 2 * f + t, :] = mean + product(mixers[t], as_rhs(field[f, t] - mean))

    def send_back(xy, carry):
        px, py = (x + xy % 4) % 4, (y + xy // 4) % 4
        column = (px * 4 + py) * 8
        for j, d in enumerate(ORDER):
            pm = column + (zl + away + d) % 8
            copy = remote(back_out.at[pm], back.at[region], a2a_send.at[2], a2a_recv.at[2], (pm, par * 2 + core))
            if j == 0:
                pl.when(xy + away > 0)(copy.start)
            else:
                copy.start()
        return carry

    lax.fori_loop(0, 16, send_back, 0)

    @pl.when(away == 0)
    def _():
        back[region] = back_out[m]

    back_wait = wait_all(back_out, back, a2a_send.at[2], a2a_recv.at[2])
    wait_recv(back_wait)
    for f in range(3):
        for t in range(2):
            out[f, pl.ds(t, 128, stride=2), :] = back[:, 2 * f + t, :]
    wait_send(height_wait)
    wait_send(wind_wait)
    wait_send(back_wait)


def local(prior, cell, value, bins):
    vmem = pl.BlockSpec(memory_space=pltpu.VMEM)
    dma = pltpu.SemaphoreType.DMA
    result = pl.pallas_call(
        kernel,
        out_shape=jax.ShapeDtypeStruct((3, 256, 128), F32),
        in_specs=[pl.BlockSpec(memory_space=pl.ANY), vmem, vmem, vmem],
        out_specs=vmem,
        scratch_shapes=[
            pltpu.VMEM((3, 256, 128), F32),
            pltpu.VMEM((2, 3, 2, ROWS, 128), F32),
            pltpu.VMEM((2, 72, 128), F32),
            pltpu.VMEM((2, 72, 128), F32),
            pltpu.VMEM((8, 128), F32),
            pltpu.VMEM((8, 128), F32),
            pltpu.VMEM((128, 2, 128), F32),
            pltpu.VMEM((128, 4, 128), F32),
            pltpu.VMEM((128, 2, 128), F32),
            pltpu.VMEM((128, 4, 128), F32),
            pltpu.VMEM((4, 72, 128), F32),
            pltpu.VMEM((3, 72, 128), F32),
            pltpu.VMEM((72, 128), F32),
            pltpu.VMEM((4, 72, 128), F32),
            pltpu.VMEM((4, 64, 128), F32),
            pltpu.VMEM((128, 6, 128), F32),
            pltpu.VMEM((128, 6, 128), F32),
            dma, dma((2,)), dma((2,)), dma, dma, dma((3,)), dma((3,)),
            dma((3,)), dma((3,)), dma((4,)), dma((4,)), dma((3,)), dma((3,)),
            pltpu.SemaphoreType.REGULAR,
        ],
        compiler_params=pltpu.CompilerParams(collective_id=0, has_side_effects=True),
    )(prior[0], cell, value, bins)
    return result[None]


def solution(mesh):
    placed = (P("mem", None, None, "slab"), P("mem", "slab"), P("mem", "slab"), P("mem", "slab"))
    return jax.shard_map(
        local, mesh=mesh, in_specs=placed, out_specs=P("mem", None, None, "slab"), check_vma=False
    )
```

time: 344 us -> 94.1 us (0.27)
  starting transfers between devices: 179 us -> 0 us
  Pallas kernels: 0 us -> 92.1 us
  waiting for transfers between devices: 80.5 us -> 0 us
  blocking collectives: 40.8 us -> 0 us
  local copies, waits for them, and re-layouts: 20.2 us -> 1.77 us
  other arithmetic: 12.4 us -> 0 us
  matrix products: 8.88 us -> 0 us
    ppermute x14 -> x0, starting transfers between devices: 111 us -> none  [the longest x8 62.6 us: passed_along(): return lax.ppermute(value, axis, pairs)]
    pallas_call x0 -> x1, Pallas kernels: none -> 92.1 us  [local(): pl.pallas_call(kernel, out_shape=jax.ShapeDtypeStruct((3, 256, 128), F32)...]
    all_to_all x2 -> x0, starting transfers between devices: 67.9 us -> none  [the longest x1 47.4 us: local(): lax.all_to_all(predicted_grid, 'mem', split_axis=2, concat_axis=0, tiled=...]
    all_to_all x1 -> x0, blocking collectives: 40.8 us -> none  [local(): lax.all_to_all(apply_weights(zone_collection, mixing), 'mem', split_axis=...]
    all_to_all x2 -> x0, waiting for transfers between devices: 40.4 us -> none  [the longest x1 23.9 us: local(): lax.all_to_all(predicted_grid, 'mem', split_axis=2, concat_axis=0, tiled=...]
    ppermute x14 -> x0, waiting for transfers between devices: 40.1 us -> none  [the longest x3 20.7 us: padded_2(): lax.ppermute(head, axis, [((i + 1) % count, i) for i in range(count)])]
    slice x92 -> x0, local copies, waits for them, and re-layouts: 12.9 us -> none  [the longest x78 11 us: east_of(): return jnp.roll(values[:, 1:-1], -1, 0)]
    dot_general x28 -> x0, matrix products: 8.88 us -> none  [the longest x23 6.27 us: batch_product(): return jnp.einsum('tij,tjk->tik', left, right, precision=highest)]
  transfers between devices with their start and end apart: 16 -> 0, of which waited for: 7 -> 0; matrix products, arithmetic and copies ran while one was open for 0% -> 0% of each run, Pallas kernels for 0% -> 0%
where the time goes in v1:
time: 94.1 us; the launch traced here: 93.9 us
  Pallas kernels  92.1 us (98%)
  local copies, waits for them, and re-layouts  1.77 us (2%)
    pallas_call x1, Pallas kernels, local(): pl.pallas_call(kernel, out_shape=jax.ShapeDtypeStruct((3, 256, 128), F32)...  92.1 us

profile of v1, /device:TPU:1, one launch (start us, length us, event | category | flops | bytes accessed | tf_op | source)
XLA Modules:
  0.0 93.9 jit_solution(575196955013270278)
XLA Ops:
  0.0 92.1 %shard_map.46 = f32[3,256,128]{2,1,0:T(8,128)} custom-call(f32[3,256,128]{2,1,0:T(8,128)} %bitcast.3, s32[1,128]{1,0:T(1,128)} %cell.1, f32[1,128]{1,0:T(1,128)} %value.1, s32[1,128]{1,0:T(1,128)} %bins.1), custom_call_target="tpu_custom_call" | custom-call | tf_op jit(solution)/shard_map/pallas_call | solution.py:411
  92.1 1.8 %copy.6 = f32[1,3,256,128]{3,2,1,0:T(8,128)} copy(f32[1,3,256,128]{3,2,1,0:T(8,128)} %bitcast.2) | data formatting | bytes 786432

commit v2 on v1

--- a/solution.py
+++ b/solution.py
@@ -88,11 +88,11 @@
 
 
 def kernel(
-    prior, cell, value, bins, out,
-    nat, state, halo_out, halo_in, obs_out, obs_in, heights_out, winds_out, heights, winds,
+    prior, cell_hbm, value_hbm, bins_hbm, out,
+    cell, value, bins, nat, state, edge, halo_out, halo_in, obs_out, obs_in, heights_out, winds_out, heights, winds,
     parts, parts_in, chunk, chunk_in, grams, back_out, back,
     load_sem, halo_send, halo_recv, obs_send, obs_recv, a2a_send, a2a_recv,
-    part_send, part_recv, chunk_send, chunk_recv, gram_send, gram_recv, lines,
+    part_send, part_recv, chunk_send, chunk_recv, gram_send, gram_recv, small_sem, lines,
 ):
     m, slab = lax.axis_index("mem"), lax.axis_index("slab")
     x, y, zl = m // 32, (m // 8) % 4, m % 8
@@ -117,6 +117,10 @@
 
     load = pltpu.make_async_copy(prior, nat, load_sem)
     load.start()
+    small = [
+        pltpu.make_async_copy(source, target, small_sem.at[i])
+        for i, (source, target) in enumerate(((cell_hbm, cell), (value_hbm, value), (bins_hbm, bins)))
+    ]
 
     barrier = pltpu.get_barrier_semaphore()
 
@@ -144,6 +148,8 @@
         return carry
 
     lax.fori_loop(1, 16, greet_line_and_plane, 0)
+    for copy in small:
+        copy.start()
     load.wait()
     for f in range(3):
         for t in range(2):
@@ -161,13 +167,29 @@
         copy.start()
     lax.fori_loop(1, 16, tell_plane, 0)
 
-    for copy in halo:
-        copy.wait()
-    for f in range(3):
-        for t in range(2):
-            i = (f * 2 + t) * 12
-            state[0, f, t, BASE + 128 : BASE + 140] = halo_in[0, i : i + 12]
-            state[0, f, t, BASE - 12 : BASE] = halo_in[1, i : i + 12]
+    def ends_at(target, side, at):
+        for f in range(3):
+            for t in range(2):
+                i = (f * 2 + t) * 12
+                target[0, f, t, at : at + 12] = halo_in[side, i : i + 12]
+
+    @pl.when(core == 0)
+    def _():
+        for f in range(3):
+            for t in range(2):
+                edge[0, f, t, 24:48] = state[0, f, t, BASE : BASE + 24]
+        halo[1].wait_send()
+        halo[0].wait_recv()
+        ends_at(state, 0, BASE + 128)
+
+    @pl.when(core == 1)
+    def _():
+        for f in range(3):
+            for t in range(2):
+                edge[0, f, t, 8:32] = state[0, f, t, BASE + 104 : BASE + 128]
+        halo[0].wait_send()
+        halo[1].wait_recv()
+        ends_at(state, 1, BASE - 12)
 
     def two_steps(counter, carry):
         for now in range(2):
@@ -177,9 +199,43 @@
 
     lax.fori_loop(0, STEPS // 2, two_steps, 0)
 
+    @pl.when(core == 0)
+    def _():
+        halo[0].wait_send()
+        halo[1].wait_recv()
+        ends_at(edge, 1, 12)
+
+    @pl.when(core == 1)
+    def _():
+        halo[1].wait_send()
+        halo[0].wait_recv()
+        ends_at(edge, 0, 32)
+
+    def two_edge_steps(counter, carry):
+        for now in range(2):
+            forecast_block(edge.at[now], edge.at[1 - now], 8, 24)
+            forecast_block(edge.at[now], edge.at[1 - now], 32, 16)
+        return carry
+
+    lax.fori_loop(0, STEPS // 2, two_edge_steps, 0)
+
+    @pl.when(core == 0)
+    def _():
+        for f in range(3):
+            for t in range(2):
+                state[0, f, t, BASE : BASE + 12] = edge[0, f, t, 24:36]
+
+    @pl.when(core == 1)
+    def _():
+        for f in range(3):
+            for t in range(2):
+                state[0, f, t, BASE + 116 : BASE + 128] = edge[0, f, t, 20:32]
+
     pl.semaphore_wait(lines, 15)
 
     ox, oy, ok = place_of(m)
+    for copy in small:
+        copy.wait()
     obs_out[0:1] = cell[...].astype(F32)
     obs_out[1:2] = value[...]
     obs_out[2:3] = bins[...].astype(F32)
@@ -411,11 +467,15 @@
     result = pl.pallas_call(
         kernel,
         out_shape=jax.ShapeDtypeStruct((3, 256, 128), F32),
-        in_specs=[pl.BlockSpec(memory_space=pl.ANY), vmem, vmem, vmem],
+        in_specs=[pl.BlockSpec(memory_space=pltpu.MemorySpace.HBM)] * 4,
         out_specs=vmem,
         scratch_shapes=[
+            pltpu.VMEM((1, 128), jnp.int32),
+            pltpu.VMEM((1, 128), F32),
+            pltpu.VMEM((1, 128), jnp.int32),
             pltpu.VMEM((3, 256, 128), F32),
             pltpu.VMEM((2, 3, 2, ROWS, 128), F32),
+            pltpu.VMEM((2, 3, 2, 56, 128), F32),
             pltpu.VMEM((2, 72, 128), F32),
             pltpu.VMEM((2, 72, 128), F32),
             pltpu.VMEM((8, 128), F32),
@@ -433,10 +493,10 @@
             pltpu.VMEM((128, 6, 128), F32),
             dma, dma((2,)), dma((2,)), dma, dma, dma((3,)), dma((3,)),
             dma((3,)), dma((3,)), dma((4,)), dma((4,)), dma((3,)), dma((3,)),
-            pltpu.SemaphoreType.REGULAR,
+            dma((3,)), pltpu.SemaphoreType.REGULAR,
         ],
-        compiler_params=pltpu.CompilerParams(collective_id=0, has_side_effects=True),
-    )(prior[0], cell, value, bins)
+        compiler_params=pltpu.CompilerParams(collective_id=0, has_side_effects=True, vmem_limit_bytes=12 * 2**20),
+    )(*(pltpu.with_memory_space_constraint(a, pltpu.MemorySpace.HBM) for a in (prior[0], cell, value, bins)))
     return result[None]
 
 

time: 94.1 us -> 89.7 us (0.953)
  Pallas kernels: 92.1 us -> 88.8 us
  local copies, waits for them, and re-layouts: 1.77 us -> 0.75 us
    pallas_call x1, Pallas kernels: 92.1 us -> 88.8 us  [local(): pl.pallas_call(kernel, out_shape=jax.ShapeDtypeStruct((3, 256, 128), F32)...]
    unnamed x1, local copies, waits for them, and re-layouts: 1.77 us -> 0.75 us
where the time goes in v2:
time: 89.7 us; the launch traced here: 89.5 us
  Pallas kernels  88.8 us (99%)
    pallas_call x1, Pallas kernels, local(): pl.pallas_call(kernel, out_shape=jax.ShapeDtypeStruct((3, 256, 128), F32)...  88.8 us

profile of v2, /device:TPU:1, one launch (start us, length us, event | category | flops | bytes accessed | tf_op | source)
XLA Modules:
  0.0 89.5 jit_solution(11208102061996188524)
XLA Ops:
  0.0 88.8 %shard_map.46 = f32[3,256,128]{2,1,0:T(8,128)S(1)} custom-call(f32[3,256,128]{2,1,0:T(8,128)} %bitcast.3, s32[1,128]{1,0:T(1,128)} %cell_hbm.1, f32[1,128]{1,0:T(1,128)} %value_hbm.1, s32[1,128]{1,0:T(1,128)} %bins_hbm.1), custom_call_target="tpu_custom_call" | custom-call | tf_op jit(solution)/shard_map/pallas_call | solution.py:467
  88.8 0.7 copy.6

commit v3 on v2

--- a/solution.py
+++ b/solution.py
@@ -10,7 +10,7 @@
 STEPS = 12
 SWEEPS = 8
 SIZE = 32
-BATCH = (16, 16, 16)
+BATCH = (8, 16, 16)
 MESH = pl.DeviceIdType.MESH
 F32 = jnp.float32
 BF16 = jnp.bfloat16

time: 89.7 us -> 87 us (0.970)
  Pallas kernels: 88.8 us -> 86.1 us
    pallas_call x1, Pallas kernels: 88.8 us -> 86.1 us  [local(): pl.pallas_call(kernel, out_shape=jax.ShapeDtypeStruct((3, 256, 128), F32)...]
where the time goes in v3:
time: 87 us; the launch traced here: 86.9 us
  Pallas kernels  86.1 us (99%)
    pallas_call x1, Pallas kernels, local(): pl.pallas_call(kernel, out_shape=jax.ShapeDtypeStruct((3, 256, 128), F32)...  86.1 us

profile of v3, /device:TPU:1, one launch (start us, length us, event | category | flops | bytes accessed | tf_op | source)
XLA Modules:
  0.0 86.9 jit_solution(11397806174238796974)
XLA Ops:
  0.0 86.1 %shard_map.46 = f32[3,256,128]{2,1,0:T(8,128)S(1)} custom-call(f32[3,256,128]{2,1,0:T(8,128)} %bitcast.3, s32[1,128]{1,0:T(1,128)} %cell_hbm.1, f32[1,128]{1,0:T(1,128)} %value_hbm.1, s32[1,128]{1,0:T(1,128)} %bins_hbm.1), custom_call_target="tpu_custom_call" | custom-call | tf_op jit(solution)/shard_map/pallas_call | solution.py:467
  86.1 0.7 copy.6
